TPU v7x, 256 devices: a whole 4x4x8 slice. The times are simulated.
256 devices in a mesh: seq: 64 (over y, z, core), tp: 4 (over x).
Axes of the slice: x: 4, y: 4, z: 8, core: 2. Of those that a mesh axis runs over, the one named last changes fastest.
Arguments:
- tokens: bfloat16 [49152, 4096], P('seq'), may hold values from -6 to 6
- query_weight: bfloat16 [4096, 2048], P('seq', 'tp'), may hold values from -0.09375 to 0.09375
- key_weight: bfloat16 [4096, 2048], P('seq', 'tp'), may hold values from -0.09375 to 0.09375
- value_weight: bfloat16 [4096, 2048], P('seq', 'tp'), may hold values from -0.09375 to 0.09375
- gate_weight: bfloat16 [4096, 16], P('seq', 'tp'), may hold values from -0.09375 to 0.09375
- decay_rate: float32 [16], P('tp'), may hold values from 4.0690106e-06 to 0.04
- norm_gain: float32 [2048], P('tp'), may hold values from 0.5 to 1.5
- out_weight: bfloat16 [2048, 4096], P(None, 'tp'), may hold values from -0.125 to 0.125
Outputs:
- mixed: bfloat16 [49152, 4096], P('seq', 'tp')
All inputs are finite; a program needn't handle non-finite values.
Results may differ from a plain program's by a relative error of at most 0.006.
The roundings to bfloat16 on the way count: a program that leaves them out, or rounds other values in their place, can miss the bound.
Values may be sent and summed in bfloat16 or wider, within the bound.
A program may use at most 128 MiB of HBM per device.

v0:
```python
import jax
import jax.numpy as jnp
from jax import lax
from jax.sharding import Mesh
from jax.sharding import PartitionSpec as P

SEQ = ("seq_0", "seq_1", "seq_2")


def side_by_side(arrays, axis, dim, along):
    both = jnp.concatenate(arrays, axis=along)
    whole, at, finished = (lax.all_gather(both, axis, axis=dim, tiled=True), 0, [])
    for a in arrays:
        finished.append(lax.slice_in_dim(whole, at, at + a.shape[along], axis=along))
        at += a.shape[along]
    return tuple(finished)


def nothing_yet(shard, identity):
    return jax.tree.map(
        lambda part, zero: jnp.zeros_like(part) + jnp.asarray(zero, part.dtype), shard, identity
    )


def carried_in(shard, axes, combine, identity):
    before = start = nothing_yet(shard, identity)
    so_far = shard
    for axis in reversed(axes):
        peers, position = (lax.axis_size(axis), lax.axis_index(axis))
        pieces = jax.tree.map(lambda part: lax.all_gather(part, axis), so_far)
        inside, so_far = (start, start)
        for k in range(peers):
            passed = k < position
            so_far = combine(so_far, jax.tree.map(lambda part: part[k], pieces))
            inside = jax.tree.map(lambda new, old: jnp.where(passed, new, old), so_far, inside)
        before = combine(inside, before)
    return before


def on_device(
    tokens, query_weight, key_weight, value_weight, gate_weight, decay_rate, norm_gain, out_weight
):
    tok_rows = tokens.shape[0]
    head_count = decay_rate.shape[0]
    proj_width = query_weight.shape[1]
    head_size = proj_width // head_count

    def contract(piece):
        return jnp.dot(tokens, piece, preferred_element_type=jnp.float32)

    pieces = side_by_side((query_weight, key_weight, value_weight, gate_weight), SEQ, 0, 1)
    query_proj, key_proj, value_proj, gate_logit = tuple(
        (contract(one_piece) for one_piece in pieces)
    )
    query_heads = query_proj.astype(jnp.bfloat16).reshape(tok_rows, head_count, head_size)
    key_heads = key_proj.astype(jnp.bfloat16).reshape(tok_rows, head_count, head_size)
    value_per_head = value_proj.astype(jnp.bfloat16).reshape(tok_rows, head_count, head_size)
    log_decay = -decay_rate[None, :] * jax.nn.softplus(gate_logit)
    within = jnp.cumsum(log_decay, axis=0)
    block_total = within[-1]
    key_scaled = (jnp.exp(block_total[None, :] - within)[:, :, None] * key_heads).astype(
        jnp.bfloat16
    )
    shard_local_state = jnp.einsum(
        "gfw,gfz->fwz", key_scaled, value_per_head, preferred_element_type=jnp.float32
    )

    def decayed_join(earlier, later):
        return (earlier[0] + later[0], jnp.exp(later[0])[:, None, None] * earlier[1] + later[1])

    _, prefix_state = carried_in(
        (block_total, shard_local_state),
        SEQ,
        decayed_join,
        (jnp.zeros_like(block_total), jnp.zeros_like(shard_local_state)),
    )
    query_scaled = (jnp.exp(within)[:, :, None] * query_heads).astype(jnp.bfloat16)
    carried_state = jnp.einsum(
        "fys,ysu->fyu",
        query_scaled,
        prefix_state.astype(jnp.bfloat16),
        preferred_element_type=jnp.float32,
    )
    scores = jnp.einsum("thk,shk->hts", query_heads, key_heads, preferred_element_type=jnp.float32)
    row_index = lax.broadcasted_iota(jnp.int32, (tok_rows, tok_rows), 0)
    col_index = lax.broadcasted_iota(jnp.int32, (tok_rows, tok_rows), 1)
    causal = (col_index <= row_index)[None, :, :]
    decay_gap = within.T[:, :, None] - within.T[:, None, :]
    attn = jnp.where(causal, scores * jnp.exp(jnp.where(causal, decay_gap, 0.0)), 0.0).astype(
        jnp.bfloat16
    )
    local_part = jnp.einsum(
        "hts,shv->thv", attn, value_per_head, preferred_element_type=jnp.float32
    )
    head_out = carried_state + local_part
    mean_square = jnp.mean(head_out * head_out, axis=-1, keepdims=True)
    normed = (head_out * lax.rsqrt(mean_square + 1e-05)).reshape(tok_rows, proj_width) * norm_gain[
        None, :
    ]
    normed = normed.astype(jnp.bfloat16)
    mixed = jnp.dot(
        lax.all_gather(normed, "tp", axis=1, tiled=True),
        out_weight,
        preferred_element_type=jnp.float32,
    )
    return mixed.astype(jnp.bfloat16)


def solution(mesh):
    finer = Mesh(mesh.devices.reshape(4, 8, 2, mesh.shape["tp"]), ("seq_0", "seq_1", "seq_2", "tp"))
    return jax.shard_map(
        on_device,
        mesh=finer,
        in_specs=(
            P(SEQ, None),
            P(SEQ, "tp"),
            P(SEQ, "tp"),
            P(SEQ, "tp"),
            P(SEQ, "tp"),
            P("tp"),
            P("tp"),
            P(None, "tp"),
        ),
        out_specs=P(SEQ, "tp"),
        check_vma=False,
    )
```

profile of v0, /device:TPU:1, one launch (start us, length us, event | category | flops | bytes accessed | tf_op | source)
XLA Modules:
  0.0 258.8 jit_solution(4576178796495780604)
XLA Ops:
  6.5 0.0 all-gather.9.cloned.1.call-start
  6.5 0.8 copy.26
  7.3 1.6 pad_maximum_fusion
  8.9 0.0 all-gather.9.cloned.1.call-update
  8.9 0.0 all-gather.11.cloned.1.call-start
  9.0 0.7 neg.9
  9.7 96.5 %all-gather.9.cloned.1.call-done = bf16[4096,1540]{1,0:T(8,128)(2,1)} async-done(((bf16[64,1540]{1,0:T(8,128)(2,1)}), bf16[4096,1540]{1,0:T(8,128)(2,1)}) %all-gather.9.cloned.1.call-update) | async-done | bytes 12615696 | tf_op jit(solution)/shard_map/all_gather | solution.py:12
  106.2 0.0 slice-start
  106.2 5.0 %fusion.70 = f32[4,768]{1,0:T(4,128)S(1)} fusion(bf16[768,4096]{1,0:T(8,128)(2,1)} %param.8, bf16[4096,1540]{1,0:T(8,128)(2,1)} %all-gather.9.cloned.1.call-done, f32[4]{0:T(128)S(1)} %neg.9), kind=kOutput, calls=%fused_computation.90 | convolution fusion | flops 25187328 | bytes 7352336 | tf_op jit(solution)/shard_map/dot_general | solution.py:49
  111.2 1.1 reduce-window.6
  112.4 0.2 slice_reduce_fusion
  112.5 0.2 reduce-window.9
  112.7 0.1 add_bitcast_fusion
  112.8 0.2 slice_reduce_fusion.1
  113.0 0.1 subtract_exponential_fusion
  113.1 0.0 slice-start.1
  113.1 7.7 %fusion.15 = bf16[512,768]{1,0:T(8,128)(2,1)S(1)} fusion(bf16[768,4096]{1,0:T(8,128)(2,1)} %param.8, bf16[4096,1540]{1,0:T(8,128)(2,1)} %all-gather.9.cloned.1.call-done), kind=kOutput, calls=%fused_computation.21 | convolution fusion | flops 3221618688 | bytes 11272192 | tf_op jit(solution)/shard_map/dot_general | solution.py:49
  120.8 0.0 slice-done
  120.8 0.0 slice-done.1
  120.8 0.0 copy-start.1
  120.8 5.9 %fusion.12 = bf16[512,768]{1,0:T(8,128)(2,1)S(1)} fusion(bf16[768,4096]{1,0:T(8,128)(2,1)S(1)} %bitcast.238, bf16[4096,1540]{1,0:T(8,128)(2,1)} %all-gather.9.cloned.1.call-done), kind=kOutput, calls=%fused_computation.20 | convolution fusion | flops 3221618688 | bytes 11272192 | tf_op jit(solution)/shard_map/dot_general | solution.py:49
  126.7 0.0 copy-start.2
  126.7 0.0 copy-done.1
  126.8 0.4 fusion.23
  127.1 2.2 all-gather
  129.3 1.8 all-gather.1
  131.1 0.0 copy-done.2
  131.1 0.8 bitcast_add_fusion.8
  131.9 0.0 all-gather.11.cloned.1.call-update
  131.9 0.0 all-gather.13.cloned.1.call-start
  132.0 0.2 iota_compare_fusion
  132.2 11.1 %all-gather.2 = f32[8,1,4]{2,1,0:T(1,128)S(1)} all-gather(f32[1,1,4]{2,1,0:T(1,128)S(1)} %get-tuple-element.23), channel_id=1, replica_groups=mesh['seq_0'=4,'seq_1'=8,'seq_2'=2,'tp'=4] {'seq_1'}, dimensions={0}, use_global_device_ids=true | all-gather | bytes 144 | tf_op jit(solution)/shard_map/all_gather | solution.py:30
  143.4 22.0 %all-gather.11.cloned.1.call-done = f32[8,4,128,128]{3,2,1,0:T(8,128)} async-done(((f32[1,4,128,128]{3,2,1,0:T(8,128)}), f32[8,4,128,128]{3,2,1,0:T(8,128)}) %all-gather.11.cloned.1.call-update) | async-done | bytes 2097168 | tf_op jit(solution)/shard_map/all_gather | solution.py:30
  165.4 2.4 multiply_add_fusion
  167.8 0.0 all-gather.13.cloned.1.call-update
  167.8 0.2 all-gather.15.cloned.1.call-start
  168.0 7.5 %fusion.18 = bf16[512,768]{1,0:T(8,128)(2,1)S(1)} fusion(bf16[768,4096]{1,0:T(8,128)(2,1)} %param.8, bf16[4096,1540]{1,0:T(8,128)(2,1)} %all-gather.9.cloned.1.call-done), kind=kOutput, calls=%fused_computation.22 | convolution fusion | flops 3221618688 | bytes 11272192 | tf_op jit(solution)/shard_map/dot_general | solution.py:49
  175.6 7.7 %all-gather.3 = f32[4,1,4]{2,1,0:T(1,128)S(1)} all-gather(f32[1,1,4]{2,1,0:T(1,128)S(1)} %get-tuple-element.10), channel_id=1, replica_groups=mesh['seq_0'=4,'seq_1'=8,'seq_2'=2,'tp'=4] {'seq_0'}, dimensions={0}, use_global_device_ids=true | all-gather | bytes 80 | tf_op jit(solution)/shard_map/all_gather | solution.py:30
  183.2 0.4 copy.28
  183.7 6.7 %fusion = f32[4,128,768]{2,1,0:T(8,128)} fusion(bf16[768,4,128]{0,2,1:T(8,128)(2,1)} %bitcast.245, f32[4,768]{1,0:T(4,128)S(1)} %get-tuple-element.9, pred[768,768]{1,0:T(8,128)(4,1)S(1)} %iota_compare_fusion, bf16[768,4,128]{0,2,1:T(8,128)(2,1)S(1)} %bitcast.240, bf16[768,4,128]{0,2,1:T(8,128)(2,1)} %bitcast.247), kind=kOutput, calls=%fused_computation.1 | convolution fusion | flops 1219756032 | bytes 4534272 | tf_op jit(solution)/shard_map/hts,shv->thv/dot_general | solution.py:92
  190.3 5.0 %all-gather.13.cloned.1.call-done = f32[4,4,128,128]{3,2,1,0:T(8,128)} async-done(((f32[1,4,128,128]{3,2,1,0:T(8,128)}), f32[4,4,128,128]{3,2,1,0:T(8,128)}) %all-gather.13.cloned.1.call-update) | async-done | bytes 1048592 | tf_op jit(solution)/shard_map/all_gather | solution.py:30
  195.3 0.0 copy-start
  195.3 3.5 %fusion.11 = (f32[768,4]{0,1:T(4,128)S(1)}, f32[4,128,768]{2,1,0:T(8,128)S(1)}) fusion(f32[4,128,768]{2,1,0:T(8,128)} %fusion, bf16[768,4,128]{2,0,1:T(8,128)(2,1)S(1)} %copy.28, f32[768,4]{0,1:T(4,128)S(1)} %get-tuple-element.8, f32[4,4,128,128]{3,2,1,0:T(8,128)} %all-gather.13.cloned.1.call-done, f32[8,4,128,128]{3,2,1,0:T(8,128)} %all-gather.11.cloned.1.call-done, ...), kind=kOutput, calls=%fused_computation.16 | convolution fusion | flops 105903104 | bytes 7627022 | tf_op jit(solution)/shard_map/fys,ysu->fyu/dot_general | solution.py:78
  198.9 0.1 bitcast_multiply_fusion.1
  199.0 0.0 copy-done
  199.0 1.0 fusion.10
  200.1 0.0 all-gather.15.cloned.1.call-update
  200.1 44.4 %all-gather.15.cloned.1.call-done = bf16[768,2048]{0,1:T(8,128)(2,1)} async-done(((bf16[768,512]{0,1:T(8,128)(2,1)}), bf16[768,2048]{0,1:T(8,128)(2,1)}) %all-gather.15.cloned.1.call-update) | async-done | bytes 3145744 | tf_op jit(solution)/shard_map/all_gather | solution.py:102
  244.5 7.8 %convolution_convert_fusion = bf16[768,1024]{1,0:T(8,128)(2,1)} fusion(bf16[768,2048]{0,1:T(8,128)(2,1)} %all-gather.15.cloned.1.call-done, bf16[2048,1024]{1,0:T(8,128)(2,1)} %param.15), kind=kOutput, calls=%fused_computation.11 | convolution fusion | flops 3222011904 | bytes 8912896 | tf_op jit(solution)/shard_map/dot_general | solution.py:101
  (10 shorter events, 0.1 us)
Async XLA Ops:
  6.5 99.7 %all-gather.9.cloned.1.call-start = ((), (), s32[]{:S(2)}) async-start(), calls=%async_computation | async-start | bytes 13844480 | tf_op jit(solution)/shard_map/all_gather | solution.py:12
  8.9 156.4 %all-gather.11.cloned.1.call-start = ((), (), s32[]{:S(2)}) async-start(), calls=%async_computation.1 | async-start | bytes 2359296 | tf_op jit(solution)/shard_map/all_gather | solution.py:30
  106.2 14.6 %slice-start = ((s8[6291456]{0:T(1024)(128)(4,1)}), s8[2097152]{0:T(1024)(128)(4,1)S(1)}, s32[]{:S(2)}) async-start(s8[6291456]{0:T(1024)(128)(4,1)} %bitcast.237), calls=%async_computation.4 | async-start | bytes 4194304
  113.1 7.7 %slice-start.1 = ((s8[6291456]{0:T(1024)(128)(4,1)}), s8[4194304]{0:T(1024)(128)(4,1)S(1)}, s32[]{:S(2)}) async-start(s8[6291456]{0:T(1024)(128)(4,1)} %bitcast.237), calls=%async_computation.5 | async-start | bytes 8388608
  120.8 6.0 %copy-start.1 = (bf16[512,768]{1,0:T(8,128)(2,1)}, bf16[512,768]{1,0:T(8,128)(2,1)S(1)}, u32[]{:S(2)}) copy-start(bf16[512,768]{1,0:T(8,128)(2,1)S(1)} %fusion.15) | copy-start | bytes 2359300
  126.7 4.4 %copy-start.2 = (bf16[512,768]{1,0:T(8,128)(2,1)}, bf16[512,768]{1,0:T(8,128)(2,1)S(1)}, u32[]{:S(2)}) copy-start(bf16[512,768]{1,0:T(8,128)(2,1)S(1)} %fusion.12) | copy-start | bytes 2359300
  131.9 63.4 %all-gather.13.cloned.1.call-start = ((), (), s32[]{:S(2)}) async-start(), calls=%async_computation.2 | async-start | bytes 1310720 | tf_op jit(solution)/shard_map/all_gather | solution.py:30
  167.8 76.7 %all-gather.15.cloned.1.call-start = ((), (), s32[]{:S(2)}) async-start(), calls=%async_computation.3 | async-start | bytes 3932160 | tf_op jit(solution)/shard_map/all_gather | solution.py:102
  195.3 3.7 %copy-start = (f32[512]{0:T(512)S(1)}, f32[512]{0:T(512)}, u32[]{:S(2)}) copy-start(f32[512]{0:T(512)} %param.14) | copy-start | bytes 6148
Sparse Core Ops, SparseCore 0:
  10.1 96.0 all-gather.8
  132.1 33.2 all-gather.10
  167.9 27.3 all-gather.12
  200.2 44.2 all-gather.14
where the time goes:
time: 259 us
  waiting for transfers between devices  168 us (65%)
  matrix products  44.5 us (17%)
  blocking collectives  22.8 us (9%)
  between operations  13.3 us (5%)
  other arithmetic  8.38 us (3%)
    all_gather x1, waiting for transfers between devices, side_by_side(): lax.all_gather(both, axis, axis=dim, tiled=True)  96.5 us
    all_gather x1, waiting for transfers between devices, on_device(): lax.all_gather(normed, 'tp', axis=1, tiled=True)  44.4 us
    all_gather x2, waiting for transfers between devices, carried_in(): pieces = jax.tree.map(lambda part: lax.all_gather(part, axis), so_far)  27 us
    dot_general x4, matrix products, contract(): return jnp.dot(tokens, piece, preferred_element_type=jnp.float32)  26.1 us
    all_gather x4, blocking collectives, carried_in(): pieces = jax.tree.map(lambda part: lax.all_gather(part, axis), so_far)  22.8 us
    dot_general x1, matrix products, on_device(): jnp.dot(lax.all_gather(normed, 'tp', axis=1, tiled=True), out_weight, pre...  7.75 us
    dot_general x1, matrix products, on_device(): jnp.einsum('hts,shv->thv', attn, value_per_head, preferred_element_type=j...  6.66 us
  transfers between devices with their start and end apart: 4, of which 4 were waited for; matrix products, arithmetic and copies ran while one was open for 6% of the time, Pallas kernels for 0%

commit v1 on v0

--- a/solution.py
+++ b/solution.py
@@ -99,7 +99,7 @@
     ]
     normed = normed.astype(jnp.bfloat16)
     mixed = jnp.dot(
-        lax.all_gather(normed, "tp", axis=1, tiled=True),
+        jnp.concatenate(lax.all_gather(normed, "tp"), axis=1),
         out_weight,
         preferred_element_type=jnp.float32,
     )

time: 259 us -> 262 us (1.012)
  local copies, waits for them, and re-layouts: 1.55 us -> 5.25 us
    all_gather x0 -> x1, local copies, waits for them, and re-layouts: none -> 3.18 us  [on_device(): lax.all_gather(normed, 'tp')]
where the time goes in v1:
time: 262 us
  waiting for transfers between devices  168 us (64%)
  matrix products  43.4 us (17%)
  blocking collectives  22.8 us (9%)
  between operations  13.4 us (5%)
  other arithmetic  8.4 us (3%)
  local copies, waits for them, and re-layouts  5.25 us (2%)
    all_gather x1, waiting for transfers between devices, side_by_side(): lax.all_gather(both, axis, axis=dim, tiled=True)  96.5 us
    all_gather x1, waiting for transfers between devices, on_device(): lax.all_gather(normed, 'tp')  44.4 us
    all_gather x2, waiting for transfers between devices, carried_in(): pieces = jax.tree.map(lambda part: lax.all_gather(part, axis), so_far)  27 us
    dot_general x4, matrix products, contract(): return jnp.dot(tokens, piece, preferred_element_type=jnp.float32)  26.1 us
    all_gather x4, blocking collectives, carried_in(): pieces = jax.tree.map(lambda part: lax.all_gather(part, axis), so_far)  22.8 us
    dot_general x1, matrix products, on_device(): jnp.dot(jnp.concatenate(lax.all_gather(normed, 'tp'), axis=1), out_weight...  6.76 us
    dot_general x1, matrix products, on_device(): jnp.einsum('hts,shv->thv', attn, value_per_head, preferred_element_type=j...  6.62 us
  transfers between devices with their start and end apart: 4, of which 4 were waited for; matrix products, arithmetic and copies ran while one was open for 6% of the time, Pallas kernels for 0%

profile of v1, /device:TPU:1, one launch (start us, length us, event | category | flops | bytes accessed | tf_op | source)
XLA Modules:
  0.0 261.5 jit_solution(9293480194204215606)
XLA Ops:
  6.5 0.0 all-gather.9.cloned.1.call-start
  6.5 0.8 copy.33
  7.3 1.6 pad_maximum_fusion
  8.9 0.0 all-gather.9.cloned.1.call-update
  8.9 0.0 all-gather.11.cloned.1.call-start
  9.0 0.7 neg.9
  9.7 96.5 %all-gather.9.cloned.1.call-done = bf16[4096,1540]{1,0:T(8,128)(2,1)} async-done(((bf16[64,1540]{1,0:T(8,128)(2,1)}), bf16[4096,1540]{1,0:T(8,128)(2,1)}) %all-gather.9.cloned.1.call-update) | async-done | bytes 12615696 | tf_op jit(solution)/shard_map/all_gather | solution.py:12
  106.2 0.0 slice-start
  106.2 5.0 %fusion.69 = f32[4,768]{1,0:T(4,128)S(1)} fusion(bf16[768,4096]{1,0:T(8,128)(2,1)} %param.8, bf16[4096,1540]{1,0:T(8,128)(2,1)} %all-gather.9.cloned.1.call-done, f32[4]{0:T(128)S(1)} %neg.9), kind=kOutput, calls=%fused_computation.89 | convolution fusion | flops 25187328 | bytes 7352336 | tf_op jit(solution)/shard_map/dot_general | solution.py:49
  111.2 1.1 reduce-window.6
  112.4 0.2 slice_reduce_fusion
  112.5 0.2 reduce-window.9
  112.7 0.1 add_bitcast_fusion
  112.8 0.2 slice_reduce_fusion.1
  113.0 0.1 subtract_exponential_fusion
  113.1 0.0 slice-start.1
  113.1 7.7 %fusion.14 = bf16[512,768]{1,0:T(8,128)(2,1)S(1)} fusion(bf16[768,4096]{1,0:T(8,128)(2,1)} %param.8, bf16[4096,1540]{1,0:T(8,128)(2,1)} %all-gather.9.cloned.1.call-done), kind=kOutput, calls=%fused_computation.20 | convolution fusion | flops 3221618688 | bytes 11272192 | tf_op jit(solution)/shard_map/dot_general | solution.py:49
  120.8 0.0 slice-done
  120.8 0.0 slice-done.1
  120.8 0.0 copy-start.1
  120.8 5.9 %fusion.11 = bf16[512,768]{1,0:T(8,128)(2,1)S(1)} fusion(bf16[768,4096]{1,0:T(8,128)(2,1)S(1)} %bitcast.239, bf16[4096,1540]{1,0:T(8,128)(2,1)} %all-gather.9.cloned.1.call-done), kind=kOutput, calls=%fused_computation.19 | convolution fusion | flops 3221618688 | bytes 11272192 | tf_op jit(solution)/shard_map/dot_general | solution.py:49
  126.7 0.0 copy-start.2
  126.7 0.0 copy-done.1
  126.8 0.4 fusion.22
  127.1 2.2 all-gather
  129.3 1.8 all-gather.1
  131.1 0.0 copy-done.2
  131.1 0.8 bitcast_add_fusion.8
  131.9 0.0 all-gather.11.cloned.1.call-update
  131.9 0.0 all-gather.13.cloned.1.call-start
  132.0 0.2 iota_compare_fusion
  132.2 11.1 %all-gather.2 = f32[8,1,4]{2,1,0:T(1,128)S(1)} all-gather(f32[1,1,4]{2,1,0:T(1,128)S(1)} %get-tuple-element.23), channel_id=1, replica_groups=mesh['seq_0'=4,'seq_1'=8,'seq_2'=2,'tp'=4] {'seq_1'}, dimensions={0}, use_global_device_ids=true | all-gather | bytes 144 | tf_op jit(solution)/shard_map/all_gather | solution.py:30
  143.4 22.0 %all-gather.11.cloned.1.call-done = f32[8,4,128,128]{3,2,1,0:T(8,128)} async-done(((f32[1,4,128,128]{3,2,1,0:T(8,128)}), f32[8,4,128,128]{3,2,1,0:T(8,128)}) %all-gather.11.cloned.1.call-update) | async-done | bytes 2097168 | tf_op jit(solution)/shard_map/all_gather | solution.py:30
  165.4 2.4 multiply_add_fusion
  167.8 0.0 all-gather.13.cloned.1.call-update
  167.8 0.2 all-gather.15.cloned.1.call-start
  168.0 7.5 %fusion.17 = bf16[512,768]{1,0:T(8,128)(2,1)S(1)} fusion(bf16[768,4096]{1,0:T(8,128)(2,1)} %param.8, bf16[4096,1540]{1,0:T(8,128)(2,1)} %all-gather.9.cloned.1.call-done), kind=kOutput, calls=%fused_computation.21 | convolution fusion | flops 3221618688 | bytes 11272192 | tf_op jit(solution)/shard_map/dot_general | solution.py:49
  175.6 7.6 %all-gather.3 = f32[4,1,4]{2,1,0:T(1,128)S(1)} all-gather(f32[1,1,4]{2,1,0:T(1,128)S(1)} %get-tuple-element.10), channel_id=1, replica_groups=mesh['seq_0'=4,'seq_1'=8,'seq_2'=2,'tp'=4] {'seq_0'}, dimensions={0}, use_global_device_ids=true | all-gather | bytes 80 | tf_op jit(solution)/shard_map/all_gather | solution.py:30
  183.2 0.4 copy.35
  183.6 6.6 %fusion = f32[4,128,768]{2,1,0:T(8,128)} fusion(bf16[768,4,128]{0,2,1:T(8,128)(2,1)} %bitcast.247, f32[4,768]{1,0:T(4,128)S(1)} %get-tuple-element.9, pred[768,768]{1,0:T(8,128)(4,1)S(1)} %iota_compare_fusion, bf16[768,4,128]{0,2,1:T(8,128)(2,1)S(1)} %bitcast.242, bf16[768,4,128]{0,2,1:T(8,128)(2,1)} %bitcast.249), kind=kOutput, calls=%fused_computation.1 | convolution fusion | flops 1219756032 | bytes 4534272 | tf_op jit(solution)/shard_map/hts,shv->thv/dot_general | solution.py:92
  190.3 5.0 %all-gather.13.cloned.1.call-done = f32[4,4,128,128]{3,2,1,0:T(8,128)} async-done(((f32[1,4,128,128]{3,2,1,0:T(8,128)}), f32[4,4,128,128]{3,2,1,0:T(8,128)}) %all-gather.13.cloned.1.call-update) | async-done | bytes 1048592 | tf_op jit(solution)/shard_map/all_gather | solution.py:30
  195.3 3.5 %fusion.10 = (f32[768,4]{0,1:T(4,128)S(1)}, f32[4,128,768]{2,1,0:T(8,128)S(1)}) fusion(f32[4,128,768]{2,1,0:T(8,128)} %fusion, bf16[768,4,128]{2,0,1:T(8,128)(2,1)S(1)} %copy.35, f32[768,4]{0,1:T(4,128)S(1)} %get-tuple-element.8, f32[4,4,128,128]{3,2,1,0:T(8,128)} %all-gather.13.cloned.1.call-done, f32[8,4,128,128]{3,2,1,0:T(8,128)} %all-gather.11.cloned.1.call-done, ...), kind=kOutput, calls=%fused_computation.14 | convolution fusion | flops 105903104 | bytes 7627022 | tf_op jit(solution)/shard_map/fys,ysu->fyu/dot_general | solution.py:78
  198.8 0.0 copy-start
  198.8 0.1 bitcast_multiply_fusion
  199.0 0.5 copy.39
  199.4 0.1 copy-done
  199.5 1.1 multiply_convert_fusion
  200.6 0.0 all-gather.15.cloned.1.call-update
  200.6 44.4 %all-gather.15.cloned.1.call-done = bf16[4,768,512]{2,1,0:T(8,128)(2,1)} async-done(((bf16[1,768,512]{2,1,0:T(8,128)(2,1)}), bf16[4,768,512]{2,1,0:T(8,128)(2,1)}) %all-gather.15.cloned.1.call-update) | async-done | bytes 3145744 | tf_op jit(solution)/shard_map/all_gather | solution.py:102
  245.0 3.2 %copy.40 = bf16[4,768,512]{1,2,0:T(8,128)(2,1)S(1)} copy(bf16[4,768,512]{2,1,0:T(8,128)(2,1)} %all-gather.15.cloned.1.call-done) | data formatting | bytes 6291456 | tf_op jit(solution)/shard_map/all_gather | solution.py:102
  248.2 6.8 %convolution_convert_fusion = bf16[768,1024]{1,0:T(8,128)(2,1)} fusion(bf16[768,2048]{0,1:T(8,128)(2,1)S(1)} %bitcast.240, bf16[2048,1024]{1,0:T(8,128)(2,1)} %param.15), kind=kOutput, calls=%fused_computation.11 | convolution fusion | flops 3222011904 | bytes 8912896 | tf_op jit(solution)/shard_map/dot_general | solution.py:101
  (10 shorter events, 0.1 us)
Async XLA Ops:
  6.5 99.7 %all-gather.9.cloned.1.call-start = ((), (), s32[]{:S(2)}) async-start(), calls=%async_computation | async-start | bytes 13844480 | tf_op jit(solution)/shard_map/all_gather | solution.py:12
  8.9 156.4 %all-gather.11.cloned.1.call-start = ((), (), s32[]{:S(2)}) async-start(), calls=%async_computation.1 | async-start | bytes 2359296 | tf_op jit(solution)/shard_map/all_gather | solution.py:30
  106.2 14.6 %slice-start = ((s8[6291456]{0:T(1024)(128)(4,1)}), s8[2097152]{0:T(1024)(128)(4,1)S(1)}, s32[]{:S(2)}) async-start(s8[6291456]{0:T(1024)(128)(4,1)} %bitcast.238), calls=%async_computation.4 | async-start | bytes 4194304
  113.1 7.7 %slice-start.1 = ((s8[6291456]{0:T(1024)(128)(4,1)}), s8[4194304]{0:T(1024)(128)(4,1)S(1)}, s32[]{:S(2)}) async-start(s8[6291456]{0:T(1024)(128)(4,1)} %bitcast.238), calls=%async_computation.5 | async-start | bytes 8388608
  120.8 6.0 %copy-start.1 = (bf16[512,768]{1,0:T(8,128)(2,1)}, bf16[512,768]{1,0:T(8,128)(2,1)S(1)}, u32[]{:S(2)}) copy-start(bf16[512,768]{1,0:T(8,128)(2,1)S(1)} %fusion.14) | copy-start | bytes 2359300
  126.7 4.4 %copy-start.2 = (bf16[512,768]{1,0:T(8,128)(2,1)}, bf16[512,768]{1,0:T(8,128)(2,1)S(1)}, u32[]{:S(2)}) copy-start(bf16[512,768]{1,0:T(8,128)(2,1)S(1)} %fusion.11) | copy-start | bytes 2359300
  131.9 63.4 %all-gather.13.cloned.1.call-start = ((), (), s32[]{:S(2)}) async-start(), calls=%async_computation.2 | async-start | bytes 1310720 | tf_op jit(solution)/shard_map/all_gather | solution.py:30
  167.8 77.2 %all-gather.15.cloned.1.call-start = ((), (), s32[]{:S(2)}) async-start(), calls=%async_computation.3 | async-start | bytes 3932160 | tf_op jit(solution)/shard_map/all_gather | solution.py:102
  198.8 0.7 copy-start
Sparse Core Ops, SparseCore 0:
  10.1 96.0 all-gather.8
  132.1 33.2 all-gather.10
  167.9 27.3 all-gather.12
  200.7 44.2 all-gather.14
